TPU v7x, 32 devices: a whole 2x2x4 slice. The times are simulated.
32 devices in a mesh: dp: 4 (over y, core), vocab: 8 (over z, x).
Axes of the slice: x: 2, y: 2, z: 4, core: 2. Of those that a mesh axis runs over, the one named last changes fastest.
Arguments:
- teacher_hidden: bfloat16 [512, 16384], P('dp', 'vocab'), may hold values from -120 to 120
- student_hidden: bfloat16 [512, 4096], P('dp', 'vocab'), may hold values from -120 to 120
- teacher_weight: bfloat16 [16384, 65536], P('dp', 'vocab'), may hold values from -1 to 1
- student_weight: bfloat16 [4096, 65536], P('dp', 'vocab'), may hold values from -1 to 1
Outputs:
- kl: float32 [512], P('dp')
- loss: float32 [], replicated
All inputs are finite; a program needn't handle non-finite values.
Results may differ from a plain program's by a relative error of at most 0.0003.
Values may be sent and summed in bfloat16 or wider, within the bound.
No kernel may reach another device: no remote copies, remote signals or barrier semaphores. Data moves between devices by JAX's collectives and lax.ppermute only.
A program may use at most 256 MiB of HBM per device.

v0:
```python
import jax
import jax.numpy as jnp
from jax import lax
from jax.sharding import PartitionSpec as P


def shards(teacher_hidden, student_hidden, teacher_weight, student_weight):
    teacher_full, student_full = (
        lax.all_gather(teacher_hidden, "vocab", axis=1, tiled=True),
        lax.all_gather(student_hidden, "vocab", axis=1, tiled=True),
    )
    tok_rows = teacher_hidden.shape[0]
    shard_vocab = teacher_weight.shape[1]
    teacher_cols, student_cols = (
        lax.all_to_all(teacher_full, "dp", split_axis=1, concat_axis=0, tiled=True),
        lax.all_to_all(student_full, "dp", split_axis=1, concat_axis=0, tiled=True),
    )
    summed = lax.psum_scatter(
        jnp.concatenate(
            [
                jnp.dot(teacher_cols, teacher_weight, preferred_element_type=jnp.float32),
                jnp.dot(student_cols, student_weight, preferred_element_type=jnp.float32),
            ],
            axis=1,
        ),
        "dp",
        scatter_dimension=0,
        tiled=True,
    )
    teacher_logit = summed[:, :shard_vocab]
    student_logit = summed[:, shard_vocab:]
    teacher_local = jnp.max(teacher_logit, axis=1)
    student_local = jnp.max(student_logit, axis=1)
    teacher_top, student_top = lax.pmax((teacher_local, student_local), "vocab")
    teacher_exp = jnp.exp(teacher_logit - teacher_top[:, None])
    teacher_total, weighted, student_total = lax.psum(
        (
            jnp.sum(teacher_exp, axis=1),
            jnp.sum(teacher_exp * (teacher_logit - student_logit), axis=1),
            jnp.sum(jnp.exp(student_logit - student_top[:, None]), axis=1),
        ),
        "vocab",
    )
    teacher_lse = teacher_top + jnp.log(teacher_total)
    student_lse = student_top + jnp.log(student_total)
    kl = weighted / teacher_total - teacher_lse + student_lse
    group_sum = lax.psum(jnp.sum(kl), "dp")
    loss = group_sum / (tok_rows * lax.axis_size("dp"))
    return (kl, loss)


def solution(mesh):
    in_specs = (P("dp", "vocab"), P("dp", "vocab"), P("dp", "vocab"), P("dp", "vocab"))
    out_specs = (P("dp"), P())
    return jax.shard_map(shards, mesh=mesh, in_specs=in_specs, out_specs=out_specs, check_vma=False)
```

profile of v0, /device:TPU:0, one launch (start us, length us, event | category | flops | bytes accessed | tf_op | source)
XLA Modules:
  0.0 567.2 jit_solution(6716977359885407873)
XLA Ops:
  7.2 0.0 all-gather.5.cloned.1.call-start
  7.2 1.7 copy.8
  8.9 0.0 all-gather.5.cloned.1.call-update
  8.9 0.0 all-gather.3.cloned.1.call-start
  8.9 2.1 copy.6
  11.0 0.0 all-gather.3.cloned.1.call-update
  11.0 42.1 %all-gather.5.cloned.1.call-done = bf16[128,4096]{0,1:T(8,128)(2,1)} async-done(((bf16[128,512]{0,1:T(8,128)(2,1)}), bf16[128,4096]{0,1:T(8,128)(2,1)}) %all-gather.5.cloned.1.call-update) | async-done | bytes 1048592 | tf_op jit(solution)/shard_map/all_gather | solution.py:10
  53.1 17.9 %all_to_all.38 = bf16[128,4,1024]{0,2,1:T(8,128)(2,1)S(1)} all-to-all(bf16[128,4,1024]{0,2,1:T(8,128)(2,1)} %bitcast.13), channel_id=1, replica_groups=mesh['dp'=4,'vocab'=8] {'dp'}, dimensions={1} | all-to-all | bytes 2097152 | tf_op jit(solution)/shard_map/all_to_all | solution.py:16
  71.0 55.8 %all-gather.3.cloned.1.call-done = bf16[128,16384]{0,1:T(8,128)(2,1)} async-done(((bf16[128,2048]{0,1:T(8,128)(2,1)}), bf16[128,16384]{0,1:T(8,128)(2,1)}) %all-gather.3.cloned.1.call-update) | async-done | bytes 4194320 | tf_op jit(solution)/shard_map/all_gather | solution.py:9
  126.8 4.8 all-to-all-start
  131.7 0.0 reduce-scatter.2.cloned.1.call-start
  131.7 0.5 copy.9
  132.2 15.6 %fusion.3 = f32[512,8192]{1,0:T(8,128)} fusion(bf16[512,1024]{1,0:T(8,128)(2,1)S(1)} %bitcast.14, bf16[1024,8192]{1,0:T(8,128)(2,1)} %param.7), kind=kOutput, calls=%fused_computation.10 | convolution fusion | flops 8589934592 | bytes 34603008 | tf_op jit(solution)/shard_map/dot_general | solution.py:22
  147.8 32.0 %all-to-all-done = bf16[128,4,4096]{0,2,1:T(8,128)(2,1)} async-done(((bf16[128,4,4096]{0,2,1:T(8,128)(2,1)}), bf16[128,4,4096]{0,2,1:T(8,128)(2,1)}, u32[]{:S(2)}, u32[]{:S(2)}) %all-to-all-start) | async-done | bytes 4194336 | tf_op jit(solution)/shard_map/all_to_all | solution.py:15
  179.9 6.4 %copy.7 = bf16[4,128,4096]{2,1,0:T(8,128)(2,1)} copy(bf16[4,128,4096]{1,2,0:T(8,128)(2,1)} %bitcast.1) | data formatting | bytes 8388608 | tf_op jit(solution)/shard_map/all_to_all | solution.py:15
  186.3 44.2 %fusion.2 = f32[512,8192]{1,0:T(8,128)} fusion(bf16[512,4096]{1,0:T(8,128)(2,1)} %bitcast.11, bf16[4096,8192]{1,0:T(8,128)(2,1)} %param.6), kind=kOutput, calls=%fused_computation.9 | convolution fusion | flops 34359738368 | bytes 88080384 | tf_op jit(solution)/shard_map/dot_general | solution.py:21
  230.5 22.5 %pad_maximum_fusion = f32[512,16384]{1,0:T(8,128)} fusion(f32[512,8192]{1,0:T(8,128)} %fusion.3, f32[512,8192]{1,0:T(8,128)} %fusion.2), kind=kLoop, calls=%fused_computation | loop fusion | flops 8388608 | bytes 67108864 | tf_op jit(solution)/shard_map/concatenate | solution.py:19
  253.0 0.0 reduce-scatter.2.cloned.1.call-update
  253.0 230.1 %reduce-scatter.2.cloned.1.call-done = f32[128,16384]{1,0:T(8,128)} async-done(((f32[512,16384]{1,0:T(8,128)}), f32[128,16384]{1,0:T(8,128)}) %reduce-scatter.2.cloned.1.call-update) | async-done | bytes 8388624 | tf_op jit(solution)/shard_map/reduce_scatter | solution.py:18
  483.1 2.5 slice_reduce_fusion.1
  485.6 21.5 %pmax.14 = f32[128]{0:T(128)S(1)} all-reduce(f32[128]{0:T(128)S(1)} %slice_reduce_fusion.1), channel_id=1, replica_groups=mesh['dp'=4,'vocab'=8] {'vocab'}, use_global_device_ids=true, to_apply=%region_2.0 | all-reduce | flops 128 | bytes 1024 | tf_op jit(solution)/shard_map/pmax | solution.py:34
  507.1 4.9 multiply_reduce_fusion
  512.0 17.1 %pmax.15 = f32[128]{0:T(128)S(1)} all-reduce(f32[128]{0:T(128)S(1)} %get-tuple-element.4), channel_id=1, replica_groups=mesh['dp'=4,'vocab'=8] {'vocab'}, use_global_device_ids=true, to_apply=%region_8.0 | all-reduce | flops 128 | bytes 1024 | tf_op jit(solution)/shard_map/pmax | solution.py:34
  529.2 2.9 exponential_reduce_fusion
  532.1 19.1 %all-reduce = (f32[128]{0:T(128)S(1)}, f32[128]{0:T(128)S(1)}, f32[128]{0:T(128)S(1)}) all-reduce(f32[128]{0:T(128)S(1)} %exponential_reduce_fusion, f32[128]{0:T(128)S(1)} %get-tuple-element.3, f32[128]{0:T(128)S(1)} %get-tuple-element.2), channel_id=1, replica_groups=mesh['dp'=4,'vocab'=8] {'vocab'}, use_global_device_ids=true, to_apply=%region_10.0 | all-reduce | flops 384 | bytes 3072 | tf_op jit(solution)/shard_map/psum | solution.py:36
  551.2 1.1 fusion.1
  552.3 6.5 %psum.31 = f32[]{:T(128)} all-reduce(f32[]{:T(128)} %get-tuple-element.8), channel_id=1, replica_groups=mesh['dp'=4,'vocab'=8] {'dp'}, use_global_device_ids=true, to_apply=%region_12.0 | all-reduce | flops 1 | bytes 8 | tf_op jit(solution)/shard_map/psum | solution.py:47
Async XLA Ops:
  7.2 46.0 %all-gather.5.cloned.1.call-start = ((), (), s32[]{:S(2)}) async-start(), calls=%async_computation.4 | async-start | bytes 1179648 | tf_op jit(solution)/shard_map/all_gather | solution.py:10
  8.9 117.9 %all-gather.3.cloned.1.call-start = ((), (), s32[]{:S(2)}) async-start(), calls=%async_computation.3 | async-start | bytes 4718592 | tf_op jit(solution)/shard_map/all_gather | solution.py:9
  126.8 53.0 %all-to-all-start = ((bf16[128,4,4096]{0,2,1:T(8,128)(2,1)}), bf16[128,4,4096]{0,2,1:T(8,128)(2,1)}, u32[]{:S(2)}, u32[]{:S(2)}) async-start(bf16[128,4,4096]{0,2,1:T(8,128)(2,1)} %bitcast.10), calls=%async_computation | async-start | bytes 8388608 | tf_op jit(solution)/shard_map/all_to_all | solution.py:15
  131.7 351.5 %reduce-scatter.2.cloned.1.call-start = ((), (), s32[]{:S(2)}) async-start(), calls=%async_computation.5 | async-start | bytes 41943040 | tf_op jit(solution)/shard_map/reduce_scatter | solution.py:18
Sparse Core Ops, SparseCore 0:
  10.1 42.9 all-gather.4
  55.3 71.5 all-gather.2
  253.2 229.9 reduce-scatter.1
where the time goes:
time: 568 us; the launch traced here: 567 us
  waiting for transfers between devices  360 us (63%)
  blocking collectives  82.3 us (14%)
  matrix products  59.8 us (11%)
  other arithmetic  33.9 us (6%)
  between operations  15.5 us (3%)
  local copies, waits for them, and re-layouts  10.7 us (2%)
    reduce_scatter x1, waiting for transfers between devices, shards(): lax.psum_scatter(jnp.concatenate([jnp.dot(teacher_cols, teacher_weight, p...  230 us
    all_gather x1, waiting for transfers between devices, shards(): lax.all_gather(teacher_hidden, 'vocab', axis=1, tiled=True)  55.8 us
    dot_general x1, matrix products, shards(): jnp.dot(teacher_cols, teacher_weight, preferred_element_type=jnp.float32)  44.2 us
    all_gather x1, waiting for transfers between devices, shards(): lax.all_gather(student_hidden, 'vocab', axis=1, tiled=True)  42.1 us
    pmax x2, blocking collectives, shards(): teacher_top, student_top = lax.pmax((teacher_local, student_local), 'vocab')  38.7 us
    all_to_all x1, waiting for transfers between devices, shards(): lax.all_to_all(teacher_full, 'dp', split_axis=1, concat_axis=0, tiled=True)  32 us
    concatenate x1, other arithmetic, shards(): jnp.concatenate([jnp.dot(teacher_cols, teacher_weight, preferred_element_...  22.5 us
    psum x1, blocking collectives, shards(): lax.psum((jnp.sum(teacher_exp, axis=1), jnp.sum(teacher_exp * (teacher_lo...  19.1 us
  transfers between devices with their start and end apart: 4, of which 4 were waited for; matrix products, arithmetic and copies ran while one was open for 3% of the time, Pallas kernels for 0%

commit v1 on v0

v1 whole, which is shorter than its diff:
```python
import functools
import math

import jax
import jax.numpy as jnp
from jax import lax
from jax.experimental import pallas as pl
from jax.experimental.pallas import tpu as pltpu
from jax.sharding import PartitionSpec as P


LANES = 128
F32 = jnp.float32
BF16 = jnp.bfloat16
SPAN, OFFSET = 248.0, 124.0
CHUNKS = {"S": (3, 5), "T": (3, 2, 2, 1)}
FIRST = (5, 3)


def block_of(n, most):
    while n % most:
        most //= 2
    return most


def assemble_kernel(where_ref, *refs, first, parts):
    *hidden, rows_ref = refs
    tok, feat = hidden[0].shape
    for i, piece in enumerate(hidden):
        row = pl.multiple_of(where_ref[2 * (first + i) + 1] * tok, tok)
        part = where_ref[2 * (first + i)]
        if parts * feat > rows_ref.shape[1]:
            part = part // 2
        for p in range(rows_ref.shape[1] // feat):

            @pl.when(part == p)
            def _(piece=piece, p=p, row=row):
                rows_ref[pl.ds(row, tok), p * feat : (p + 1) * feat] = piece[...]


def assemble(where, hidden, first, slots, parts):
    tok, feat = hidden[0].shape
    return pl.pallas_call(
        functools.partial(assemble_kernel, first=first, parts=parts),
        in_specs=[pl.BlockSpec(memory_space=pltpu.SMEM)]
        + [pl.BlockSpec(memory_space=pltpu.VMEM)] * len(hidden),
        out_specs=pl.BlockSpec(memory_space=pltpu.VMEM),
        out_shape=jax.ShapeDtypeStruct((slots * tok, len(hidden) * feat // slots), BF16),
        compiler_params=pltpu.CompilerParams(vmem_limit_bytes=12 * 2**20),
    )(where, *hidden)


def spans(width, shares):
    edges = [width * sum(shares[:i]) // sum(shares) for i in range(len(shares) + 1)]
    return [(a, b - a) for a, b in zip(edges, edges[1:])]


def holder(chunks, start):
    return max(i for i, (first, _) in enumerate(chunks) if first <= start)


def matmul_kernel(which_ref, rows_ref, *refs, count, base, split):
    weights = refs[:count]
    outs = refs[count + base :]
    feat = weights[0].shape[0]
    total = refs[count][...] if base else None
    for i, weight in enumerate(weights):
        dot = jnp.dot(
            rows_ref[:, i * feat : (i + 1) * feat], weight[...], preferred_element_type=F32
        )
        total = dot if total is None else total + dot
    if split:
        half = total.shape[0] // 2
        outs[0][...] = total[:half]
        outs[1][...] = total[half:]
    else:
        outs[0][...] = total


def matmul(which, rows, weight, start, width, bn, parts=1, base=None, split=True):
    count, depth = rows.shape
    bn = block_of(math.gcd(width, start, base[1] if base else 0), bn)
    blocks = max(parts // 2, 1)
    feat = depth // blocks
    specs = [pl.BlockSpec((count, depth), lambda j, w: (0, 0))]
    for i in range(blocks):
        specs.append(
            pl.BlockSpec(
                (feat, bn),
                lambda j, w, i=i: ((2 * i + w[0]) if parts > 1 else 0, start // bn + j),
            )
        )
    args = [rows] + [weight] * blocks
    if base is not None:
        specs.append(pl.BlockSpec((count, bn), lambda j, w: (0, base[1] // bn + j)))
        args.append(base[0])
    outs = 2 if split else 1
    return pl.pallas_call(
        functools.partial(
            matmul_kernel, count=blocks, base=int(base is not None), split=split
        ),
        grid_spec=pltpu.PrefetchScalarGridSpec(
            num_scalar_prefetch=1,
            grid=(width // bn,),
            in_specs=specs,
            out_specs=[pl.BlockSpec((count // outs, bn), lambda j, w: (0, j))] * outs,
        ),
        out_shape=[jax.ShapeDtypeStruct((count // outs, width), F32)] * outs,
        compiler_params=pltpu.CompilerParams(
            dimension_semantics=("arbitrary",), vmem_limit_bytes=24 * 2**20
        ),
        cost_estimate=pl.CostEstimate(
            flops=2 * count * depth * width,
            bytes_accessed=2 * depth * width + 4 * count * width,
            transcendentals=0,
        ),
    )(which, *args)


def encode_kernel(keep_ref, recv_ref, code_ref, own_ref):
    rows, width = code_ref.shape[0], keep_ref.shape[1]
    value = keep_ref[:rows] + recv_ref[:rows]
    size = jnp.abs(value)
    top = jnp.max(size, axis=1, keepdims=True)
    scale = jnp.maximum(top * 1.01, 1e-30).astype(BF16)
    power = jnp.exp2(size * (SPAN / scale.astype(F32)) - OFFSET)
    code_ref[:, :width] = jnp.where(value < 0.0, -power, power).astype(BF16)
    code_ref[:, width:] = jnp.broadcast_to(scale, (rows, LANES))
    own_ref[...] = keep_ref[rows:] + recv_ref[rows:]


def encode(keep, recv, tok, bn):
    total, width = keep.shape
    rows = total - tok
    steps = width // bn
    return pl.pallas_call(
        encode_kernel,
        grid=(steps,),
        in_specs=[pl.BlockSpec((total, bn), lambda j: (0, j))] * 2,
        out_specs=[
            pl.BlockSpec((rows, bn + LANES), lambda j: (0, j)),
            pl.BlockSpec((tok, bn), lambda j: (0, j)),
        ],
        out_shape=[
            jax.ShapeDtypeStruct((rows, steps * (bn + LANES)), BF16),
            jax.ShapeDtypeStruct((tok, width), F32),
        ],
        compiler_params=pltpu.CompilerParams(
            dimension_semantics=("arbitrary",), vmem_limit_bytes=24 * 2**20
        ),
        cost_estimate=pl.CostEstimate(
            flops=8 * total * width,
            bytes_accessed=12 * total * width,
            transcendentals=rows * width,
        ),
    )(keep, recv)


def decoded(code, scale):
    power = code.astype(F32)
    size = (jnp.log2(jnp.abs(power)) + OFFSET) * (scale.astype(F32) * (1.0 / SPAN))
    return jnp.where(power < 0.0, -size, size)


def own_logits(own_ref, codes):
    total = own_ref[...]
    bn = total.shape[1]
    for code in codes:
        width = code.shape[1] - LANES
        column = pl.multiple_of(pl.program_id(0) * bn % width, LANES)
        total += decoded(code[:, pl.ds(column, bn)], code[:, width : width + 1])
    return total


def columns_of(old, columns):
    lane = lax.broadcasted_iota(jnp.int32, old.shape, 1)
    new = old
    for i, column in columns.items():
        new = jnp.where(lane == i, column, new)
    return new


def student_kernel(own_ref, *refs, others):
    codes = refs[:others]
    prev_ref, logit_ref, out_ref = refs[others:]

    @pl.when(pl.program_id(0) == 0)
    def _():
        out_ref[...] = prev_ref[...]

    s = own_logits(own_ref, codes)
    logit_ref[...] = s
    old = out_ref[...]
    top = jnp.maximum(old[:, 3:4], jnp.max(s, axis=1, keepdims=True))
    total = old[:, 4:5] * jnp.exp(old[:, 3:4] - top) + jnp.sum(
        jnp.exp(s - top), axis=1, keepdims=True
    )
    out_ref[...] = columns_of(old, {3: top, 4: total})


def teacher_kernel(own_ref, *refs, others, last):
    codes = refs[:others]
    logit_ref, prev_ref, out_ref, acc_ref = refs[others:]
    step = pl.program_id(0)

    @pl.when(step == 0)
    def _():
        acc_ref[...] = prev_ref[...]

    t = own_logits(own_ref, codes)
    old = acc_ref[...]
    top = jnp.maximum(old[:, 0:1], jnp.max(t, axis=1, keepdims=True))
    size = jnp.exp(t - top)
    fade = jnp.exp(old[:, 0:1] - top)
    total = old[:, 1:2] * fade + jnp.sum(size, axis=1, keepdims=True)
    weighted = old[:, 2:3] * fade + jnp.sum(size * (t - logit_ref[...]), axis=1, keepdims=True)
    new = columns_of(old, {0: top, 1: total, 2: weighted})
    acc_ref[...] = new

    @pl.when(step == pl.num_programs(0) - 1)
    def _():
        if last:
            out_ref[...] = jnp.transpose(new)[:8]
        else:
            out_ref[...] = new


def stats(chunk, tok, prev, logit=None, start=0, last=False):
    own, codes, code_block = chunk
    width = own.shape[1]
    bn = block_of(math.gcd(code_block, start), 1024)
    per = code_block // bn
    whole = pl.BlockSpec((tok, LANES), lambda j: (0, 0))
    specs = [pl.BlockSpec((tok, bn), lambda j: (0, j))]
    specs += [pl.BlockSpec((tok, code_block + LANES), lambda j: (0, j // per))] * len(codes)
    args = [own, *codes]
    scratch = []
    if logit is None:
        kernel = functools.partial(student_kernel, others=len(codes))
        out_specs = [pl.BlockSpec((tok, bn), lambda j: (0, j)), whole]
        out_shape = [
            jax.ShapeDtypeStruct((tok, width), F32),
            jax.ShapeDtypeStruct((tok, LANES), F32),
        ]
    else:
        kernel = functools.partial(teacher_kernel, others=len(codes), last=last)
        specs.append(pl.BlockSpec((tok, bn), lambda j: (0, start // bn + j)))
        args.append(logit)
        shape = (8, tok) if last else (tok, LANES)
        out_specs = pl.BlockSpec(shape, lambda j: (0, 0))
        out_shape = jax.ShapeDtypeStruct(shape, F32)
        scratch = [pltpu.VMEM((tok, LANES), F32)]
    return pl.pallas_call(
        kernel,
        grid=(width // bn,),
        in_specs=specs + [whole],
        out_specs=out_specs,
        out_shape=out_shape,
        scratch_shapes=scratch,
        compiler_params=pltpu.CompilerParams(
            dimension_semantics=("arbitrary",), vmem_limit_bytes=14 * 2**20
        ),
        cost_estimate=pl.CostEstimate(
            flops=20 * tok * width, bytes_accessed=14 * tok * width, transcendentals=2 * tok * width
        ),
    )(*args, prev)


def merge(a, b):
    t_top, s_top = jnp.maximum(a[0:1], b[0:1]), jnp.maximum(a[3:4], b[3:4])
    ta, tb = jnp.exp(a[0:1] - t_top), jnp.exp(b[0:1] - t_top)
    sa, sb = jnp.exp(a[3:4] - s_top), jnp.exp(b[3:4] - s_top)
    return jnp.concatenate(
        [t_top, a[1:3] * ta + b[1:3] * tb, s_top, a[4:5] * sa + b[4:5] * sb, a[5:8]], axis=0
    )


def shards(teacher_hidden, student_hidden, teacher_weight, student_weight):
    nd, nv = lax.axis_size("dp"), lax.axis_size("vocab")
    chips = nd // 2
    r = nv // nd
    ring = nv // 2
    tok = teacher_hidden.shape[0]
    vocab = teacher_weight.shape[1]
    d, v = lax.axis_index("dp"), lax.axis_index("vocab")

    def place(group):
        return (group % 2) * chips + group // 2

    shuffle = [
        (g * nv + f, (f // r) * nv + place(g) * r + f % r) for g in range(nd) for f in range(nv)
    ]
    turn = [(i, (i + 2) % nv) for i in range(nv)]
    flip = [(i, i ^ 1) for i in range(nv)]

    where = []
    for b in range(2):
        for k in range(ring):
            j = ((v // 2 - k) % ring) * 2 + (v % 2) ^ b
            group, part = j // r, j % r
            core, chip = group // chips, group % chips
            ahead = (chip - d // 2 - 1) % chips
            slot = jnp.where(core == d % 2, chips, 0) + ahead
            where += [part, slot]
    where = jnp.stack(where).astype(jnp.int32)

    parity = jnp.reshape(v % 2, (1,)).astype(jnp.int32)
    partner = [(i, i ^ 1) for i in range(nd)]

    def across(code):
        codes = []
        for o in range(1, chips):
            to = [(y * 2 + c, ((y + o) % chips) * 2 + c) for y in range(chips) for c in range(2)]
            codes.append(lax.ppermute(code[(o - 1) * tok : o * tok], "dp", to))
        return codes

    def gather(hidden):
        pieces = [lax.ppermute(hidden, ("dp", "vocab"), shuffle)]
        flips = []
        for k in range(ring):
            flips.append(lax.ppermute(pieces[k], "vocab", flip))
            if k < ring - 1:
                pieces.append(lax.ppermute(pieces[k], "vocab", turn))
        return pieces, flips

    def exchange(send, keep):
        width = keep.shape[1]
        steps = -(-width // 3072)
        while width % (steps * LANES):
            steps += 1
        code_block = width // steps
        recv = lax.ppermute(send, "dp", partner)
        code, own = encode(keep, recv, tok, code_block)
        return own, across(code), code_block

    student, teacher = [], []
    turns, flips = gather(student_hidden)
    student_weight = pltpu.with_memory_space_constraint(student_weight, pltpu.HBM)
    rows = assemble(where, turns + flips, 0, nd, r)
    s_spans = spans(vocab, CHUNKS["S"])
    for start, width in s_spans:
        send, keep = matmul(parity, rows, student_weight, start, width, 1024)
        student.append(exchange(send, keep))

    turns, flips = gather(teacher_hidden)
    rows = assemble(where, turns, 0, nd, r)
    bases = []
    b_spans = spans(vocab, FIRST)
    for start, width in b_spans:
        bases += matmul(parity, rows, teacher_weight, start, width, 512, parts=r, split=False)
    rows = assemble(where, flips, ring, nd, r)
    t_spans = spans(vocab, CHUNKS["T"])
    for start, width in t_spans:
        k = holder(b_spans, start)
        base = (bases[k], start - b_spans[k][0])
        send, keep = matmul(1 - parity, rows, teacher_weight, start, width, 512, parts=r, base=base)
        teacher.append(exchange(send, keep))

    lane = lax.broadcasted_iota(jnp.int32, (tok, LANES), 1)
    run = jnp.where((lane == 0) | (lane == 3), -3.0e38, 0.0).astype(F32)
    logits = []
    for chunk in student:
        logit, run = stats(chunk, tok, run)
        logits.append(logit)
    for i, chunk in enumerate(teacher):
        k = holder(s_spans, t_spans[i][0])
        start = t_spans[i][0] - s_spans[k][0]
        run = stats(chunk, tok, run, logits[k], start, i == len(teacher) - 1)

    bit = 1
    while bit < nv:
        run = merge(run, lax.ppermute(run, "vocab", [(i, i ^ bit) for i in range(nv)]))
        bit *= 2
    kl = run[2] / run[1] - (run[0] + jnp.log(run[1])) + (run[3] + jnp.log(run[4]))
    loss = lax.psum(jnp.sum(kl), "dp") / (tok * nd)
    return (kl, loss)


def solution(mesh):
    spec = P("dp", "vocab")

    return jax.shard_map(
        shards, mesh=mesh, in_specs=(spec,) * 4, out_specs=(P("dp"), P()), check_vma=False
    )
```

time: 568 us -> 295 us (0.52)
  waiting for transfers between devices: 360 us -> 125 us
  Pallas kernels: 0 us -> 102 us
  blocking collectives: 82.3 us -> 6.36 us
  matrix products: 59.8 us -> 0 us
  starting transfers between devices: 4.97 us -> 52.9 us
  other arithmetic: 33.9 us -> 1.21 us
  between operations: 15.5 us -> 2.72 us
  local copies, waits for them, and re-layouts: 10.7 us -> 3.48 us
    reduce_scatter x1 -> x0, waiting for transfers between devices: 230 us -> none  [shards(): lax.psum_scatter(jnp.concatenate([jnp.dot(teacher_cols, teacher_weight, p...]
    ppermute x0 -> x31, waiting for transfers between devices: none -> 125 us  [the longest x6 73.5 us: across(): codes.append(lax.ppermute(code[(o - 1) * tok:o * tok], 'dp', to))]
    pallas_call x0 -> x23, Pallas kernels: none -> 102 us  [the longest x8 75.1 us: matmul(): pl.pallas_call(functools.partial(matmul_kernel, count=blocks, base=int(ba...]
    all_gather x2 -> x0, waiting for transfers between devices: 97.9 us -> none  [the longest x1 55.8 us: shards(): lax.all_gather(teacher_hidden, 'vocab', axis=1, tiled=True)]
    dot_general x2 -> x0, matrix products: 59.8 us -> none  [the longest x1 44.2 us: shards(): jnp.dot(teacher_cols, teacher_weight, preferred_element_type=jnp.float32)]
    ppermute x0 -> x31, starting transfers between devices: none -> 52.9 us  [the longest x6 28.6 us: gather(): pieces.append(lax.ppermute(pieces[k], 'vocab', turn))]
    pmax x2 -> x0, blocking collectives: 38.7 us -> none  [shards(): teacher_top, student_top = lax.pmax((teacher_local, student_local), 'vocab')]
    all_to_all x1 -> x0, waiting for transfers between devices: 32 us -> none  [shards(): lax.all_to_all(teacher_full, 'dp', split_axis=1, concat_axis=0, tiled=True)]
  transfers between devices with their start and end apart: 4 -> 31, of which waited for: 4 -> 18; matrix products, arithmetic and copies ran while one was open for 3% -> 0% of each run, Pallas kernels for 0% -> 35%
where the time goes in v1:
time: 295 us; the launch traced here: 294 us
  waiting for transfers between devices  125 us (42%)
  Pallas kernels  102 us (35%)
  starting transfers between devices  52.9 us (18%)
  blocking collectives  6.36 us (2%)
  local copies, waits for them, and re-layouts  3.48 us (1%)
    pallas_call x8, Pallas kernels, matmul(): pl.pallas_call(functools.partial(matmul_kernel, count=blocks, base=int(ba...  75.1 us
    ppermute x6, waiting for transfers between devices, across(): codes.append(lax.ppermute(code[(o - 1) * tok:o * tok], 'dp', to))  73.5 us
    ppermute x6, starting transfers between devices, gather(): pieces.append(lax.ppermute(pieces[k], 'vocab', turn))  28.6 us
    ppermute x6, waiting for transfers between devices, gather(): pieces.append(lax.ppermute(pieces[k], 'vocab', turn))  27.3 us
    ppermute x8, waiting for transfers between devices, gather(): flips.append(lax.ppermute(pieces[k], 'vocab', flip))  18 us
    pallas_call x6, Pallas kernels, stats(): pl.pallas_call(kernel, grid=(width // bn,), in_specs=specs + [whole], out...  12.8 us
    pallas_call x6, Pallas kernels, encode(): pl.pallas_call(encode_kernel, grid=(steps,), in_specs=[pl.BlockSpec((tota...  11.7 us
    ppermute x8, starting transfers between devices, gather(): flips.append(lax.ppermute(pieces[k], 'vocab', flip))  10 us
  transfers between devices with their start and end apart: 31, of which 18 were waited for; matrix products, arithmetic and copies ran while one was open for 0% of the time, Pallas kernels for 35%

profile of v1, /device:TPU:0, one launch (start us, length us, event | category | flops | bytes accessed | tf_op | source)
XLA Modules:
  0.0 294.4 jit_solution(2803376600232673239)
XLA Ops:
  3.9 25.6 %collective-permute-start.11 = (bf16[128,512]{1,0:T(8,128)(2,1)S(1)}, bf16[128,512]{1,0:T(8,128)(2,1)S(1)}, u32[]{:S(2)}, u32[]{:S(2)}) collective-permute-start(bf16[128,512]{1,0:T(8,128)(2,1)S(1)} %collective-permute-done.10.refs_0_), channel_id=1, source_target_pairs={{0,2},{1,3},{2,4},{3,5},{4,6},{5,7},{6,0},{7,1},{8,10},{9,11},{10,... | collective-permute-start | bytes 393224 | tf_op jit(solution)/shard_map/ppermute | solution.py:323
  29.5 3.9 %collective-permute-done.11.refs_1_ = bf16[128,512]{1,0:T(8,128)(2,1)S(1)} collective-permute-done((bf16[128,512]{1,0:T(8,128)(2,1)S(1)}, bf16[128,512]{1,0:T(8,128)(2,1)S(1)}, u32[]{:S(2)}, u32[]{:S(2)}) %collective-permute-start.11) | collective-permute-done | bytes 131104 | tf_op jit(solution)/shard_map/ppermute | solution.py:323
  33.4 2.5 collective-permute-start.12
  35.9 13.0 %collective-permute-done.12.refs_2_ = bf16[128,512]{1,0:T(8,128)(2,1)S(1)} collective-permute-done((bf16[128,512]{1,0:T(8,128)(2,1)S(1)}, bf16[128,512]{1,0:T(8,128)(2,1)S(1)}, u32[]{:S(2)}, u32[]{:S(2)}) %collective-permute-start.12) | collective-permute-done | bytes 131104 | tf_op jit(solution)/shard_map/ppermute | solution.py:323
  52.9 3.6 %collective-permute-done.13.refs_3_ = bf16[128,512]{1,0:T(8,128)(2,1)S(1)} collective-permute-done((bf16[128,512]{1,0:T(8,128)(2,1)S(1)}, bf16[128,512]{1,0:T(8,128)(2,1)S(1)}, u32[]{:S(2)}, u32[]{:S(2)}) %collective-permute-start.13) | collective-permute-done | bytes 131104 | tf_op jit(solution)/shard_map/ppermute | solution.py:323
  58.5 2.8 collective-permute-done.16.refs_6_
  63.9 10.2 %shard_map.65 = (f32[256,5120]{1,0:T(8,128)}, f32[256,5120]{1,0:T(8,128)S(1)}) custom-call(s32[1]{0:T(128)} %bitcast.which_ref, bf16[512,1024]{1,0:T(8,128)(2,1)S(1)} %shard_map.64.rows_ref, bf16[1024,8192]{1,0:T(8,128)(2,1)} %refs_0_.11), custom_call_target="tpu_custom_call" | custom-call | flops 5368709120 | bytes 20971520 | tf_op jit(solution)/shard_map/pallas_call | solution.py:98
  74.1 4.9 %collective-permute-done.4.refs_2_ = bf16[128,2048]{1,0:T(8,128)(2,1)S(1)} collective-permute-done((bf16[128,2048]{1,0:T(8,128)(2,1)}, bf16[128,2048]{1,0:T(8,128)(2,1)S(1)}, u32[]{:S(2)}, u32[]{:S(2)}) %collective-permute-start.4) | collective-permute-done | bytes 524320 | tf_op jit(solution)/shard_map/ppermute | solution.py:323
  80.5 7.0 %shard_map.67 = (f32[256,3072]{1,0:T(8,128)}, f32[256,3072]{1,0:T(8,128)S(1)}) custom-call(s32[1]{0:T(128)} %bitcast.which_ref, bf16[512,1024]{1,0:T(8,128)(2,1)S(1)} %shard_map.64.rows_ref, bf16[1024,8192]{1,0:T(8,128)(2,1)} %refs_0_.11), custom_call_target="tpu_custom_call" | custom-call | flops 3221225472 | bytes 12582912 | tf_op jit(solution)/shard_map/pallas_call | solution.py:98
  95.7 16.1 %shard_map.73.refs_1_ = f32[512,5120]{1,0:T(8,128)S(1)} custom-call(s32[1]{0:T(128)} %bitcast.which_ref, bf16[512,2048]{1,0:T(8,128)(2,1)S(1)} %shard_map.60.rows_ref, bf16[4096,8192]{1,0:T(8,128)(2,1)} %refs_0_.15), custom_call_target="tpu_custom_call" | custom-call | flops 10737418240 | bytes 31457280 | tf_op jit(solution)/shard_map/pallas_call | solution.py:98
  111.9 3.4 %collective-permute-done.5.refs_2_ = bf16[128,2048]{1,0:T(8,128)(2,1)S(1)} collective-permute-done((bf16[128,2048]{1,0:T(8,128)(2,1)S(1)}, bf16[128,2048]{1,0:T(8,128)(2,1)S(1)}, u32[]{:S(2)}, u32[]{:S(2)}) %collective-permute-start.5) | collective-permute-done | bytes 524320 | tf_op jit(solution)/shard_map/ppermute | solution.py:321
  115.4 9.6 %collective-permute-done.7.refs_3_ = bf16[128,2048]{1,0:T(8,128)(2,1)S(1)} collective-permute-done((bf16[128,2048]{1,0:T(8,128)(2,1)S(1)}, bf16[128,2048]{1,0:T(8,128)(2,1)S(1)}, u32[]{:S(2)}, u32[]{:S(2)}) %collective-permute-start.7) | collective-permute-done | bytes 524320 | tf_op jit(solution)/shard_map/ppermute | solution.py:321
  125.8 11.1 %shard_map.76 = (f32[256,3072]{1,0:T(8,128)}, f32[256,3072]{1,0:T(8,128)S(1)}) custom-call(s32[1]{0:T(128)S(6)} %sub.175.which_ref, bf16[512,2048]{1,0:T(8,128)(2,1)S(1)} %shard_map.59.rows_ref, bf16[4096,8192]{1,0:T(8,128)(2,1)} %refs_0_.15, f32[512,5120]{1,0:T(8,128)S(1)} %shard_map.73.refs_1_), custom_call_target="tpu_custom_call" | custom-call | flops 6442450944 | bytes 18874368 | tf_op jit(solution)/shard_map/pallas_call | solution.py:98
  138.6 10.2 %shard_map.61.refs_1_ = f32[512,3072]{1,0:T(8,128)S(1)} custom-call(s32[1]{0:T(128)} %bitcast.which_ref, bf16[512,2048]{1,0:T(8,128)(2,1)S(1)} %shard_map.60.rows_ref, bf16[4096,8192]{1,0:T(8,128)(2,1)} %refs_0_.15), custom_call_target="tpu_custom_call" | custom-call | flops 6442450944 | bytes 18874368 | tf_op jit(solution)/shard_map/pallas_call | solution.py:98
  148.8 8.0 %shard_map.74 = (f32[256,2048]{1,0:T(8,128)}, f32[256,2048]{1,0:T(8,128)S(1)}) custom-call(s32[1]{0:T(128)S(6)} %sub.175.which_ref, bf16[512,2048]{1,0:T(8,128)(2,1)S(1)} %shard_map.59.rows_ref, bf16[4096,8192]{1,0:T(8,128)(2,1)} %refs_0_.15, f32[512,5120]{1,0:T(8,128)S(1)} %shard_map.73.refs_1_), custom_call_target="tpu_custom_call" | custom-call | flops 4294967296 | bytes 12582912 | tf_op jit(solution)/shard_map/pallas_call | solution.py:98
  157.4 7.6 %shard_map.71 = (f32[256,2048]{1,0:T(8,128)S(1)}, f32[256,2048]{1,0:T(8,128)S(1)}) custom-call(s32[1]{0:T(128)S(6)} %sub.175.which_ref, bf16[512,2048]{1,0:T(8,128)(2,1)S(1)} %shard_map.59.rows_ref, bf16[4096,8192]{1,0:T(8,128)(2,1)} %refs_0_.15, f32[512,3072]{1,0:T(8,128)S(1)} %shard_map.61.refs_1_), custom_call_target="tpu_custom_call" | custom-call | flops 4294967296 | bytes 12582912 | tf_op jit(solution)/shard_map/pallas_call | solution.py:98
  165.6 4.9 %shard_map.62 = (f32[256,1024]{1,0:T(8,128)}, f32[256,1024]{1,0:T(8,128)S(1)}) custom-call(s32[1]{0:T(128)S(6)} %sub.175.which_ref, bf16[512,2048]{1,0:T(8,128)(2,1)S(1)} %shard_map.59.rows_ref, bf16[4096,8192]{1,0:T(8,128)(2,1)} %refs_0_.15, f32[512,3072]{1,0:T(8,128)S(1)} %shard_map.61.refs_1_), custom_call_target="tpu_custom_call" | custom-call | flops 2147483648 | bytes 6291456 | tf_op jit(solution)/shard_map/pallas_call | solution.py:98
  170.5 4.0 %shard_map.66 = (bf16[128,5376]{1,0:T(8,128)(2,1)S(1)}, f32[128,5120]{1,0:T(8,128)S(1)}) custom-call(f32[256,5120]{1,0:T(8,128)S(1)} %get-tuple-element.34.keep_ref, f32[256,5120]{1,0:T(8,128)} %collective-permute-done.18.recv_ref), custom_call_target="tpu_custom_call" | custom-call | flops 10485760 | bytes 15728640 | tf_op jit(solution)/shard_map/pallas_call | solution.py:136
  174.6 3.0 %shard_map.68 = (bf16[128,3200]{1,0:T(8,128)(2,1)S(1)}, f32[128,3072]{1,0:T(8,128)S(1)}) custom-call(f32[256,3072]{1,0:T(8,128)S(1)} %copy-done.1, f32[256,3072]{1,0:T(8,128)} %collective-permute-done.20.recv_ref), custom_call_target="tpu_custom_call" | custom-call | flops 6291456 | bytes 9437184 | tf_op jit(solution)/shard_map/pallas_call | solution.py:136
  177.6 2.1 collective-permute-start.21
  179.7 3.0 %shard_map.77 = (bf16[128,3200]{1,0:T(8,128)(2,1)S(1)}, f32[128,3072]{1,0:T(8,128)S(1)}) custom-call(f32[256,3072]{1,0:T(8,128)S(1)} %copy-done.3, f32[256,3072]{1,0:T(8,128)} %collective-permute-done.26.recv_ref), custom_call_target="tpu_custom_call" | custom-call | flops 6291456 | bytes 9437184 | tf_op jit(solution)/shard_map/pallas_call | solution.py:136
  183.5 2.1 collective-permute-start.25
  186.7 38.5 %collective-permute-done.21.refs_0_ = bf16[128,3200]{1,0:T(8,128)(2,1)S(1)} collective-permute-done((bf16[128,3200]{1,0:T(8,128)(2,1)S(1)}, bf16[128,3200]{1,0:T(8,128)(2,1)S(1)}, u32[]{:S(2)}, u32[]{:S(2)}) %collective-permute-start.21) | collective-permute-done | bytes 819232 | tf_op jit(solution)/shard_map/ppermute | solution.py:314
  227.1 5.5 %shard_map.70 = (f32[128,5120]{1,0:T(8,128)S(1)}, f32[128,128]{1,0:T(8,128)S(1)}) custom-call(f32[128,5120]{1,0:T(8,128)S(1)} %get-tuple-element.36.own_ref, bf16[128,5376]{1,0:T(8,128)(2,1)S(1)} %collective-permute-done.19.refs_0_, f32[128,128]{1,0:T(8,128)S(1)} %get-tuple-element.42.refs_1_), custom_call_target="tpu_custom_call" | custom-call | flops 13107200 | bytes 9175040 | tf_op jit(solution)/shard_map/pallas_call | solution.py:253
  232.6 10.1 %collective-permute-done.27.refs_0_ = bf16[128,3200]{1,0:T(8,128)(2,1)S(1)} collective-permute-done((bf16[128,3200]{1,0:T(8,128)(2,1)S(1)}, bf16[128,3200]{1,0:T(8,128)(2,1)S(1)}, u32[]{:S(2)}, u32[]{:S(2)}) %collective-permute-start.27) | collective-permute-done | bytes 819232 | tf_op jit(solution)/shard_map/ppermute | solution.py:314
  244.8 9.9 %collective-permute-done.25.refs_0_ = bf16[128,2176]{1,0:T(8,128)(2,1)S(1)} collective-permute-done((bf16[128,2176]{1,0:T(8,128)(2,1)S(1)}, bf16[128,2176]{1,0:T(8,128)(2,1)S(1)}, u32[]{:S(2)}, u32[]{:S(2)}) %collective-permute-start.25) | collective-permute-done | bytes 557088 | tf_op jit(solution)/shard_map/ppermute | solution.py:314
  256.1 10.5 %collective-permute-done.23.refs_0_ = bf16[128,2176]{1,0:T(8,128)(2,1)S(1)} collective-permute-done((bf16[128,2176]{1,0:T(8,128)(2,1)S(1)}, bf16[128,2176]{1,0:T(8,128)(2,1)S(1)}, u32[]{:S(2)}, u32[]{:S(2)}) %collective-permute-start.23) | collective-permute-done | bytes 557088 | tf_op jit(solution)/shard_map/ppermute | solution.py:314
  268.0 4.4 %collective-permute-done.9.refs_0_ = bf16[128,1152]{1,0:T(8,128)(2,1)S(1)} collective-permute-done((bf16[128,1152]{1,0:T(8,128)(2,1)S(1)}, bf16[128,1152]{1,0:T(8,128)(2,1)S(1)}, u32[]{:S(2)}, u32[]{:S(2)}) %collective-permute-start.9) | collective-permute-done | bytes 294944 | tf_op jit(solution)/shard_map/ppermute | solution.py:314
  274.6 2.1 collective-permute-done.28
  280.5 2.1 collective-permute-start.30
  282.7 2.4 collective-permute-done.30
  286.2 6.4 %psum.7 = f32[]{:T(128)} all-reduce(f32[]{:T(128)} %get-tuple-element.58), channel_id=1, replica_groups=mesh['dp'=4,'vocab'=8] {'dp'}, use_global_device_ids=true, to_apply=%region_1.2 | all-reduce | flops 1 | bytes 8 | tf_op jit(solution)/shard_map/psum | solution.py:375
  (81 shorter events, 41.1 us)
Async XLA Ops:
  0.6 28.9 %collective-permute-start = (bf16[128,2048]{1,0:T(8,128)(2,1)}, bf16[128,2048]{1,0:T(8,128)(2,1)S(1)}, u32[]{:S(2)}, u32[]{:S(2)}) collective-permute-start(bf16[128,2048]{1,0:T(8,128)(2,1)} %param.4), channel_id=1, source_target_pairs={{0,0},{1,1},{2,8},{3,9},{4,16},{5,17},{6,24},{7,25},{8,4},{9,5},{1... | collective-permute-start | bytes 1572872 | tf_op jit(solution)/shard_map/ppermute | solution.py:318
  2.3 1.6 collective-permute-start.10
  3.9 29.5 %collective-permute-start.11 = (bf16[128,512]{1,0:T(8,128)(2,1)S(1)}, bf16[128,512]{1,0:T(8,128)(2,1)S(1)}, u32[]{:S(2)}, u32[]{:S(2)}) collective-permute-start(bf16[128,512]{1,0:T(8,128)(2,1)S(1)} %collective-permute-done.10.refs_0_), channel_id=1, source_target_pairs={{0,2},{1,3},{2,4},{3,5},{4,6},{5,7},{6,0},{7,1},{8,10},{9,11},{10,... | collective-permute-start | bytes 393224 | tf_op jit(solution)/shard_map/ppermute | solution.py:323
  29.5 34.3 %collective-permute-start.2 = (bf16[128,2048]{1,0:T(8,128)(2,1)S(1)}, bf16[128,2048]{1,0:T(8,128)(2,1)}, u32[]{:S(2)}, u32[]{:S(2)}) collective-permute-start(bf16[128,2048]{1,0:T(8,128)(2,1)S(1)} %collective-permute-done.refs_0_), channel_id=1, source_target_pairs={{0,2},{1,3},{2,4},{3,5},{4,6},{5,7},{6,0},{7,1},{8,10},{9,11},{10,... | collective-permute-start | bytes 1572872 | tf_op jit(solution)/shard_map/ppermute | solution.py:323
  33.4 15.5 %collective-permute-start.12 = (bf16[128,512]{1,0:T(8,128)(2,1)S(1)}, bf16[128,512]{1,0:T(8,128)(2,1)S(1)}, u32[]{:S(2)}, u32[]{:S(2)}) collective-permute-start(bf16[128,512]{1,0:T(8,128)(2,1)S(1)} %collective-permute-done.11.refs_1_), channel_id=1, source_target_pairs={{0,2},{1,3},{2,4},{3,5},{4,6},{5,7},{6,0},{7,1},{8,10},{9,11},{10,... | collective-permute-start | bytes 393224 | tf_op jit(solution)/shard_map/ppermute | solution.py:323
  48.9 7.6 %collective-permute-start.13 = (bf16[128,512]{1,0:T(8,128)(2,1)S(1)}, bf16[128,512]{1,0:T(8,128)(2,1)S(1)}, u32[]{:S(2)}, u32[]{:S(2)}) collective-permute-start(bf16[128,512]{1,0:T(8,128)(2,1)S(1)} %collective-permute-done.12.refs_2_), channel_id=1, source_target_pairs={{0,2},{1,3},{2,4},{3,5},{4,6},{5,7},{6,0},{7,1},{8,10},{9,11},{10,... | collective-permute-start | bytes 393224 | tf_op jit(solution)/shard_map/ppermute | solution.py:323
  49.4 8.7 %collective-permute-start.14 = (bf16[128,512]{1,0:T(8,128)(2,1)S(1)}, bf16[128,512]{1,0:T(8,128)(2,1)S(1)}, u32[]{:S(2)}, u32[]{:S(2)}) collective-permute-start(bf16[128,512]{1,0:T(8,128)(2,1)S(1)} %collective-permute-done.10.refs_0_), channel_id=1, source_target_pairs={{0,1},{1,0},{2,3},{3,2},{4,5},{5,4},{6,7},{7,6},{8,9},{9,8},{10,11... | collective-permute-start | bytes 393224 | tf_op jit(solution)/shard_map/ppermute | solution.py:321
  50.8 7.7 %collective-permute-start.15 = (bf16[128,512]{1,0:T(8,128)(2,1)S(1)}, bf16[128,512]{1,0:T(8,128)(2,1)S(1)}, u32[]{:S(2)}, u32[]{:S(2)}) collective-permute-start(bf16[128,512]{1,0:T(8,128)(2,1)S(1)} %collective-permute-done.11.refs_1_), channel_id=1, source_target_pairs={{0,1},{1,0},{2,3},{3,2},{4,5},{5,4},{6,7},{7,6},{8,9},{9,8},{10,11... | collective-permute-start | bytes 393224 | tf_op jit(solution)/shard_map/ppermute | solution.py:321
  51.4 10.0 %collective-permute-start.16 = (bf16[128,512]{1,0:T(8,128)(2,1)S(1)}, bf16[128,512]{1,0:T(8,128)(2,1)S(1)}, u32[]{:S(2)}, u32[]{:S(2)}) collective-permute-start(bf16[128,512]{1,0:T(8,128)(2,1)S(1)} %collective-permute-done.12.refs_2_), channel_id=1, source_target_pairs={{0,1},{1,0},{2,3},{3,2},{4,5},{5,4},{6,7},{7,6},{8,9},{9,8},{10,11... | collective-permute-start | bytes 393224 | tf_op jit(solution)/shard_map/ppermute | solution.py:321
  56.5 6.6 %collective-permute-start.17 = (bf16[128,512]{1,0:T(8,128)(2,1)S(1)}, bf16[128,512]{1,0:T(8,128)(2,1)S(1)}, u32[]{:S(2)}, u32[]{:S(2)}) collective-permute-start(bf16[128,512]{1,0:T(8,128)(2,1)S(1)} %collective-permute-done.13.refs_3_), channel_id=1, source_target_pairs={{0,1},{1,0},{2,3},{3,2},{4,5},{5,4},{6,7},{7,6},{8,9},{9,8},{10,11... | collective-permute-start | bytes 393224 | tf_op jit(solution)/shard_map/ppermute | solution.py:321
  63.8 15.1 %collective-permute-start.4 = (bf16[128,2048]{1,0:T(8,128)(2,1)}, bf16[128,2048]{1,0:T(8,128)(2,1)S(1)}, u32[]{:S(2)}, u32[]{:S(2)}) collective-permute-start(bf16[128,2048]{1,0:T(8,128)(2,1)} %collective-permute-done.2.refs_1_), channel_id=1, source_target_pairs={{0,2},{1,3},{2,4},{3,5},{4,6},{5,7},{6,0},{7,1},{8,10},{9,11},{10,... | collective-permute-start | bytes 1572872 | tf_op jit(solution)/shard_map/ppermute | solution.py:323
  74.1 96.4 %collective-permute-start.18 = (f32[256,5120]{1,0:T(8,128)}, f32[256,5120]{1,0:T(8,128)}, u32[]{:S(2)}, u32[]{:S(2)}) collective-permute-start(f32[256,5120]{1,0:T(8,128)} %get-tuple-element.35), channel_id=1, source_target_pairs={{0,8},{8,0},{16,24},{24,16},{1,9},{9,1},{17,25},{25,17},{2,10},{10... | collective-permute-start | bytes 15728648 | tf_op jit(solution)/shard_map/ppermute | solution.py:332
  79.0 14.0 %collective-permute-start.6 = (bf16[128,2048]{1,0:T(8,128)(2,1)S(1)}, bf16[128,2048]{1,0:T(8,128)(2,1)S(1)}, u32[]{:S(2)}, u32[]{:S(2)}) collective-permute-start(bf16[128,2048]{1,0:T(8,128)(2,1)S(1)} %collective-permute-done.4.refs_2_), channel_id=1, source_target_pairs={{0,2},{1,3},{2,4},{3,5},{4,6},{5,7},{6,0},{7,1},{8,10},{9,11},{10,... | collective-permute-start | bytes 1572872 | tf_op jit(solution)/shard_map/ppermute | solution.py:323
  79.0 32.9 %collective-permute-start.1 = (bf16[128,2048]{1,0:T(8,128)(2,1)S(1)}, bf16[128,2048]{1,0:T(8,128)(2,1)S(1)}, u32[]{:S(2)}, u32[]{:S(2)}) collective-permute-start(bf16[128,2048]{1,0:T(8,128)(2,1)S(1)} %collective-permute-done.refs_0_), channel_id=1, source_target_pairs={{0,1},{1,0},{2,3},{3,2},{4,5},{5,4},{6,7},{7,6},{8,9},{9,8},{10,11... | collective-permute-start | bytes 1572872 | tf_op jit(solution)/shard_map/ppermute | solution.py:321
  89.1 22.8 %collective-permute-start.3 = (bf16[128,2048]{1,0:T(8,128)(2,1)}, bf16[128,2048]{1,0:T(8,128)(2,1)S(1)}, u32[]{:S(2)}, u32[]{:S(2)}) collective-permute-start(bf16[128,2048]{1,0:T(8,128)(2,1)} %collective-permute-done.2.refs_1_), channel_id=1, source_target_pairs={{0,1},{1,0},{2,3},{3,2},{4,5},{5,4},{6,7},{7,6},{8,9},{9,8},{10,11... | collective-permute-start | bytes 1572872 | tf_op jit(solution)/shard_map/ppermute | solution.py:321
  89.6 25.7 %collective-permute-start.5 = (bf16[128,2048]{1,0:T(8,128)(2,1)S(1)}, bf16[128,2048]{1,0:T(8,128)(2,1)S(1)}, u32[]{:S(2)}, u32[]{:S(2)}) collective-permute-start(bf16[128,2048]{1,0:T(8,128)(2,1)S(1)} %collective-permute-done.4.refs_2_), channel_id=1, source_target_pairs={{0,1},{1,0},{2,3},{3,2},{4,5},{5,4},{6,7},{7,6},{8,9},{9,8},{10,11... | collective-permute-start | bytes 1572872 | tf_op jit(solution)/shard_map/ppermute | solution.py:321
  93.0 31.9 %collective-permute-start.7 = (bf16[128,2048]{1,0:T(8,128)(2,1)S(1)}, bf16[128,2048]{1,0:T(8,128)(2,1)S(1)}, u32[]{:S(2)}, u32[]{:S(2)}) collective-permute-start(bf16[128,2048]{1,0:T(8,128)(2,1)S(1)} %collective-permute-done.6.refs_3_), channel_id=1, source_target_pairs={{0,1},{1,0},{2,3},{3,2},{4,5},{5,4},{6,7},{7,6},{8,9},{9,8},{10,11... | collective-permute-start | bytes 1572872 | tf_op jit(solution)/shard_map/ppermute | solution.py:321
  111.9 62.7 %collective-permute-start.20 = (f32[256,3072]{1,0:T(8,128)}, f32[256,3072]{1,0:T(8,128)}, u32[]{:S(2)}, u32[]{:S(2)}) collective-permute-start(f32[256,3072]{1,0:T(8,128)} %get-tuple-element.39), channel_id=1, source_target_pairs={{0,8},{8,0},{16,24},{24,16},{1,9},{9,1},{17,25},{25,17},{2,10},{10... | collective-permute-start | bytes 9437192 | tf_op jit(solution)/shard_map/ppermute | solution.py:332
  138.6 39.0 %collective-permute-start.26 = (f32[256,3072]{1,0:T(8,128)}, f32[256,3072]{1,0:T(8,128)}, u32[]{:S(2)}, u32[]{:S(2)}) collective-permute-start(f32[256,3072]{1,0:T(8,128)} %get-tuple-element.53), channel_id=1, source_target_pairs={{0,8},{8,0},{16,24},{24,16},{1,9},{9,1},{17,25},{25,17},{2,10},{10... | collective-permute-start | bytes 9437192 | tf_op jit(solution)/shard_map/ppermute | solution.py:332
  156.9 8.1 %copy-start.4 = (f32[256,2048]{1,0:T(8,128)}, f32[256,2048]{1,0:T(8,128)S(1)}, u32[]{:S(2)}) copy-start(f32[256,2048]{1,0:T(8,128)S(1)} %get-tuple-element.48.keep_ref) | copy-start | bytes 6291460
  156.9 25.8 %collective-permute-start.24 = (f32[256,2048]{1,0:T(8,128)}, f32[256,2048]{1,0:T(8,128)S(1)}, u32[]{:S(2)}, u32[]{:S(2)}) collective-permute-start(f32[256,2048]{1,0:T(8,128)} %get-tuple-element.49), channel_id=1, source_target_pairs={{0,8},{8,0},{16,24},{24,16},{1,9},{9,1},{17,25},{25,17},{2,10},{10... | collective-permute-start | bytes 6291464 | tf_op jit(solution)/shard_map/ppermute | solution.py:332
  164.9 18.5 %collective-permute-start.22 = (f32[256,2048]{1,0:T(8,128)S(1)}, f32[256,2048]{1,0:T(8,128)S(1)}, u32[]{:S(2)}, u32[]{:S(2)}) collective-permute-start(f32[256,2048]{1,0:T(8,128)S(1)} %get-tuple-element.45), channel_id=1, source_target_pairs={{0,8},{8,0},{16,24},{24,16},{1,9},{9,1},{17,25},{25,17},{2,10},{10... | collective-permute-start | bytes 6291464 | tf_op jit(solution)/shard_map/ppermute | solution.py:332
  170.5 15.8 %collective-permute-start.8 = (f32[256,1024]{1,0:T(8,128)}, f32[256,1024]{1,0:T(8,128)S(1)}, u32[]{:S(2)}, u32[]{:S(2)}) collective-permute-start(f32[256,1024]{1,0:T(8,128)} %get-tuple-element.31), channel_id=1, source_target_pairs={{0,8},{8,0},{16,24},{24,16},{1,9},{9,1},{17,25},{25,17},{2,10},{10... | collective-permute-start | bytes 3145736 | tf_op jit(solution)/shard_map/ppermute | solution.py:332
  174.5 52.5 %collective-permute-start.19 = (bf16[128,5376]{1,0:T(8,128)(2,1)S(1)}, bf16[128,5376]{1,0:T(8,128)(2,1)S(1)}, u32[]{:S(2)}, u32[]{:S(2)}) collective-permute-start(bf16[128,5376]{1,0:T(8,128)(2,1)S(1)} %get-tuple-element.37), channel_id=1, source_target_pairs={{0,16},{8,24},{16,0},{24,8},{1,17},{9,25},{17,1},{25,9},{2,18},{10... | collective-permute-start | bytes 4128776 | tf_op jit(solution)/shard_map/ppermute | solution.py:314
  177.6 47.6 %collective-permute-start.21 = (bf16[128,3200]{1,0:T(8,128)(2,1)S(1)}, bf16[128,3200]{1,0:T(8,128)(2,1)S(1)}, u32[]{:S(2)}, u32[]{:S(2)}) collective-permute-start(bf16[128,3200]{1,0:T(8,128)(2,1)S(1)} %get-tuple-element.41), channel_id=1, source_target_pairs={{0,16},{8,24},{16,0},{24,8},{1,17},{9,25},{17,1},{25,9},{2,18},{10... | collective-permute-start | bytes 2457608 | tf_op jit(solution)/shard_map/ppermute | solution.py:314
  182.7 60.0 %collective-permute-start.27 = (bf16[128,3200]{1,0:T(8,128)(2,1)S(1)}, bf16[128,3200]{1,0:T(8,128)(2,1)S(1)}, u32[]{:S(2)}, u32[]{:S(2)}) collective-permute-start(bf16[128,3200]{1,0:T(8,128)(2,1)S(1)} %get-tuple-element.55), channel_id=1, source_target_pairs={{0,16},{8,24},{16,0},{24,8},{1,17},{9,25},{17,1},{25,9},{2,18},{10... | collective-permute-start | bytes 2457608 | tf_op jit(solution)/shard_map/ppermute | solution.py:314
  183.5 71.2 %collective-permute-start.25 = (bf16[128,2176]{1,0:T(8,128)(2,1)S(1)}, bf16[128,2176]{1,0:T(8,128)(2,1)S(1)}, u32[]{:S(2)}, u32[]{:S(2)}) collective-permute-start(bf16[128,2176]{1,0:T(8,128)(2,1)S(1)} %get-tuple-element.51), channel_id=1, source_target_pairs={{0,16},{8,24},{16,0},{24,8},{1,17},{9,25},{17,1},{25,9},{2,18},{10... | collective-permute-start | bytes 1671176 | tf_op jit(solution)/shard_map/ppermute | solution.py:314
  186.2 80.4 %collective-permute-start.23 = (bf16[128,2176]{1,0:T(8,128)(2,1)S(1)}, bf16[128,2176]{1,0:T(8,128)(2,1)S(1)}, u32[]{:S(2)}, u32[]{:S(2)}) collective-permute-start(bf16[128,2176]{1,0:T(8,128)(2,1)S(1)} %get-tuple-element.47), channel_id=1, source_target_pairs={{0,16},{8,24},{16,0},{24,8},{1,17},{9,25},{17,1},{25,9},{2,18},{10... | collective-permute-start | bytes 1671176 | tf_op jit(solution)/shard_map/ppermute | solution.py:314
  225.2 47.3 %collective-permute-start.9 = (bf16[128,1152]{1,0:T(8,128)(2,1)S(1)}, bf16[128,1152]{1,0:T(8,128)(2,1)S(1)}, u32[]{:S(2)}, u32[]{:S(2)}) collective-permute-start(bf16[128,1152]{1,0:T(8,128)(2,1)S(1)} %get-tuple-element.33), channel_id=1, source_target_pairs={{0,16},{8,24},{16,0},{24,8},{1,17},{9,25},{17,1},{25,9},{2,18},{10... | collective-permute-start | bytes 884744 | tf_op jit(solution)/shard_map/ppermute | solution.py:314
  273.1 3.6 %collective-permute-start.28 = (f32[8,128]{1,0:T(8,128)S(1)}, f32[8,128]{1,0:T(8,128)S(1)}, u32[]{:S(2)}, u32[]{:S(2)}) collective-permute-start(f32[8,128]{1,0:T(8,128)S(1)} %shard_map.81), channel_id=1, source_target_pairs={{0,1},{1,0},{2,3},{3,2},{4,5},{5,4},{6,7},{7,6},{8,9},{9,8},{10,11... | collective-permute-start | bytes 12296 | tf_op jit(solution)/shard_map/ppermute | solution.py:372
  276.8 3.7 %collective-permute-start.29 = (f32[8,128]{1,0:T(8,128)S(1)}, f32[8,128]{1,0:T(8,128)S(1)}, u32[]{:S(2)}, u32[]{:S(2)}) collective-permute-start(f32[8,128]{1,0:T(8,128)S(1)} %concatenate.6), channel_id=1, source_target_pairs={{0,2},{1,3},{2,0},{3,1},{4,6},{5,7},{6,4},{7,5},{8,10},{9,11},{10,... | collective-permute-start | bytes 12296 | tf_op jit(solution)/shard_map/ppermute | solution.py:372
  280.5 4.6 %collective-permute-start.30 = (f32[8,128]{1,0:T(8,128)S(1)}, f32[8,128]{1,0:T(8,128)S(1)}, u32[]{:S(2)}, u32[]{:S(2)}) collective-permute-start(f32[8,128]{1,0:T(8,128)S(1)} %concatenate.7), channel_id=1, source_target_pairs={{0,4},{1,5},{2,6},{3,7},{4,0},{5,1},{6,2},{7,3},{8,12},{9,13},{10,... | collective-permute-start | bytes 12296 | tf_op jit(solution)/shard_map/ppermute | solution.py:372
  (5 other events, 15.6 us)
